TPU v7x, 512 devices: a whole 4x4x16 slice. The times are simulated.
512 devices in a mesh: dp: 128 (over z, x, core), mp: 4 (over y).
Axes of the slice: x: 4, y: 4, z: 16, core: 2. Of those that a mesh axis runs over, the one named last changes fastest.
Arguments:
- grad_blocks: bfloat16 [256, 128, 128], P('dp', None, 'mp'), may hold values from -0.5 to 0.5
- owner_table: int32 [256], replicated, may hold values from 0 to 127, as said below
- prev_stats: float32 [1024, 2, 128, 128], P('dp'), as said below
Outputs:
- update: bfloat16 [256, 128, 128], P('dp', None, 'mp')
- new_stats: float32 [1024, 2, 128, 128], P('dp')
- inv_roots: float32 [1024, 2, 128, 128], P('dp')
Inputs may be any that keep to these rules, and one draw needn't show every extreme that they name: `owner_table`: every entry is a dp index; no index appears more than 8 times, and some index appears exactly 8 times. `prev_stats`: each [128, 128] matrix is symmetric positive semidefinite.
All inputs are finite; a program needn't handle non-finite values.
Results may differ from a plain program's by a relative error of at most 0.001.
Values may be sent and summed in bfloat16 or wider, within the bound.
A program may use at most 64 MiB of HBM per device.

v0:
```python
import jax
import jax.numpy as jnp
from jax import lax
from jax.sharding import PartitionSpec as P

ITERS = 16
STAT_DECAY = 0.75
DAMPING = 0.03


def batch_product(first, second):
    return jnp.einsum("pij,pjk->pik", first, second, precision=lax.Precision.HIGHEST)


def newton_roots(matrices):
    width = matrices.shape[-1]
    identity = jnp.eye(width, dtype=jnp.float32)
    trace_val = jnp.trace(matrices, axis1=1, axis2=2)
    damped = matrices + DAMPING / width * trace_val[:, None, None] * identity
    norm_val = jnp.sqrt(jnp.sum(damped * damped, axis=(1, 2)))
    root_mat = identity * (1.0 / jnp.sqrt(jnp.sqrt(norm_val)))[:, None, None]
    remainder = damped / norm_val[:, None, None]

    def refine(unused, state_pair):
        root_now, rest_now = state_pair
        factor = (5.0 * identity - rest_now) * 0.25
        root_now = batch_product(root_now, factor)
        square = batch_product(factor, factor)
        quartic = batch_product(square, square)
        return (root_now, batch_product(quartic, rest_now))

    root_mat, remainder = lax.fori_loop(0, ITERS, refine, (root_mat, remainder))
    return root_mat


def per_device(grad_blocks, owner_table, prev_stats):
    dev_count = lax.axis_size("dp")
    my_index = lax.axis_index("dp")
    part_count = lax.axis_size("mp")
    part_index = lax.axis_index("mp")
    blk_local = grad_blocks.shape[0]
    width = grad_blocks.shape[1]
    part_width = grad_blocks.shape[2]
    capacity = prev_stats.shape[0]
    block_total = owner_table.shape[0]
    home_owner = lax.dynamic_slice_in_dim(owner_table, my_index * blk_local, blk_local)
    send_mask = jnp.arange(dev_count, dtype=jnp.int32)[:, None] == home_owner[None, :]
    owned_mask = (owner_table == my_index).astype(jnp.int32)
    slot_rank = jnp.cumsum(owned_mask) - owned_mask
    slot_range = jnp.arange(capacity, dtype=jnp.int32)
    picker = ((owned_mask[None, :] == 1) & (slot_rank[None, :] == slot_range[:, None])).astype(
        jnp.bfloat16
    )
    filled = slot_range < jnp.sum(owned_mask)

    def route(blocks):
        return jnp.where(send_mask[:, :, None, None], blocks[None], jnp.zeros((), blocks.dtype))

    def pick(arrived):
        flat = arrived.reshape(block_total, -1)
        chosen = jnp.dot(picker, flat, preferred_element_type=jnp.float32)
        return chosen.astype(jnp.bfloat16).reshape((capacity,) + arrived.shape[2:])

    arrived = lax.all_to_all(route(grad_blocks), "dp", split_axis=0, concat_axis=0, tiled=True)
    whole = lax.all_gather(pick(arrived), "mp", axis=2, tiled=True)
    left_stat = jnp.einsum("rik,rjk->rij", whole, whole, preferred_element_type=jnp.float32)
    right_stat = jnp.einsum("rki,rkj->rij", whole, whole, preferred_element_type=jnp.float32)
    blended = STAT_DECAY * prev_stats + (1.0 - STAT_DECAY) * jnp.stack(
        [left_stat, right_stat], axis=1
    )
    new_stats = jnp.where(filled[:, None, None, None], blended, 0.0)
    identity = jnp.eye(width, dtype=jnp.float32)
    problems = jnp.where(filled[:, None, None, None], blended, identity).reshape(
        2 * capacity, width, width
    )
    share = 2 * capacity // part_count
    my_problems = lax.dynamic_slice_in_dim(problems, part_index * share, share, 0)
    roots_flat = lax.all_gather(newton_roots(my_problems), "mp", axis=0, tiled=True)
    roots = roots_flat.reshape(capacity, 2, width, width)
    inv_roots = jnp.where(filled[:, None, None, None], roots, 0.0)
    whole_wide = whole.astype(jnp.float32)
    precond = jnp.einsum("rij,rjk->rik", roots[:, 0], whole_wide, precision=lax.Precision.HIGHEST)
    precond = jnp.einsum("rij,rjk->rik", precond, roots[:, 1], precision=lax.Precision.HIGHEST)
    spread = jnp.sqrt(jnp.mean(precond * precond, axis=(1, 2)))
    spread = jnp.where(filled, spread, 1.0)
    scaled = (precond / spread[:, None, None]).astype(jnp.bfloat16)
    columns = lax.dynamic_slice_in_dim(scaled, part_index * part_width, part_width, 2)
    outgoing = jnp.dot(picker.T, columns.reshape(capacity, -1), preferred_element_type=jnp.float32)
    outgoing = outgoing.astype(jnp.bfloat16).reshape(dev_count, blk_local, width, part_width)
    returned = lax.all_to_all(outgoing, "dp", split_axis=0, concat_axis=0, tiled=True)
    update = returned[home_owner, jnp.arange(blk_local, dtype=jnp.int32)]
    return (update, new_stats, inv_roots)


def solution(mesh):
    return jax.shard_map(
        per_device,
        mesh=mesh,
        in_specs=(P("dp", None, "mp"), P(), P("dp", None, None, None)),
        out_specs=(P("dp", None, "mp"), P("dp", None, None, None), P("dp", None, None, None)),
        check_vma=False,
    )
```

profile of v0, /device:TPU:33, one launch (start us, length us, event | category | flops | bytes accessed | tf_op | source)
XLA Modules:
  0.0 361.8 jit_solution(6509518457858769847)
XLA Ops:
  7.2 0.8 fusion.27
  7.9 2.3 broadcast_select_fusion
  10.2 19.4 %all-to-all-start = ((bf16[128,2,128,32]{2,3,1,0:T(8,128)(2,1)}), bf16[128,2,128,32]{2,3,1,0:T(8,128)(2,1)S(1)}, u32[]{:S(2)}, u32[]{:S(2)}) async-start(bf16[128,2,128,32]{2,3,1,0:T(8,128)(2,1)} %broadcast_select_fusion), calls=%async_computation | async-start | bytes 4194304 | tf_op jit(solution)/shard_map/all_to_all | solution.py:64
  30.3 0.6 fusion.28
  30.9 0.6 iota_compare_fusion.4
  31.6 97.5 %all-to-all-done = bf16[128,2,128,32]{2,3,1,0:T(8,128)(2,1)S(1)} async-done(((bf16[128,2,128,32]{2,3,1,0:T(8,128)(2,1)}), bf16[128,2,128,32]{2,3,1,0:T(8,128)(2,1)S(1)}, u32[]{:S(2)}, u32[]{:S(2)}) %all-to-all-start) | async-done | bytes 2097184 | tf_op jit(solution)/shard_map/all_to_all | solution.py:64
  129.1 6.5 %copy.32 = bf16[128,2,128,32]{3,2,1,0:T(8,128)(2,1)} copy(bf16[128,2,128,32]{2,3,1,0:T(8,128)(2,1)S(1)} %all-to-all-done) | data formatting | bytes 4194304 | tf_op jit(solution)/shard_map/all_to_all | solution.py:64
  135.6 10.7 %reshape.97 = bf16[256,4096]{1,0:T(8,128)(2,1)S(1)} reshape(bf16[128,2,128,32]{3,2,1,0:T(8,128)(2,1)} %copy.32) | data formatting | bytes 4194304 | tf_op jit(solution)/shard_map/reshape | solution.py:60
  146.9 10.7 %all_gather.6 = bf16[8,128,128]{1,2,0:T(8,128)(2,1)S(1)} all-gather(bf16[8,128,32]{1,2,0:T(8,128)(2,1)S(1)} %copy.33), channel_id=1, replica_groups=mesh['dp'=128,'mp'=4] {'mp'}, dimensions={2}, use_global_device_ids=true | all-gather | bytes 327680 | tf_op jit(solution)/shard_map/all_gather | solution.py:65
  159.2 29.6 %while.13 = (s32[]{:T(128)}, f32[4,128,128]{1,2,0:T(8,128)S(1)}, f32[4,128,128]{2,1,0:T(8,128)S(1)}, s32[]{:T(128)}) while((s32[]{:T(128)}, f32[4,128,128]{1,2,0:T(8,128)S(1)}, f32[4,128,128]{2,1,0:T(8,128)S(1)}, s32[]{:T(128)}) %tuple.39), condition=%wide.region_6.7_spmd.clone, body=%wide.region_5.6_spmd.clone.sunk | while | flops 402948096 | bytes 3866677 | solution.py:32
  160.1 0.6 convolution_bitcast_fusion.4
  161.9 0.6 convolution_bitcast_fusion.4
  163.8 0.6 convolution_bitcast_fusion.4
  164.4 0.4 fusion.64
  165.6 0.6 convolution_bitcast_fusion.4
  166.2 0.4 fusion.64
  167.5 0.6 convolution_bitcast_fusion.4
  169.3 0.6 convolution_bitcast_fusion.4
  169.9 0.4 fusion.64
  171.1 0.6 convolution_bitcast_fusion.4
  171.8 0.4 fusion.64
  173.0 0.6 convolution_bitcast_fusion.4
  174.8 0.6 convolution_bitcast_fusion.4
  176.7 0.6 convolution_bitcast_fusion.4
  177.3 0.4 fusion.64
  178.5 0.6 convolution_bitcast_fusion.4
  180.4 0.6 convolution_bitcast_fusion.4
  181.0 0.4 fusion.64
  182.2 0.6 convolution_bitcast_fusion.4
  184.1 0.6 convolution_bitcast_fusion.4
  185.9 0.6 convolution_bitcast_fusion.4
  187.8 0.6 convolution_bitcast_fusion.4
  188.4 0.4 fusion.64
  188.8 0.8 copy.36
  189.7 23.8 %all-gather.2.cloned.1.call-done = f32[16,128,128]{2,1,0:T(8,128)} async-done(((f32[4,128,128]{2,1,0:T(8,128)}), f32[16,128,128]{2,1,0:T(8,128)}) %all-gather.2.cloned.1.call-update) | async-done | bytes 1048592 | tf_op jit(solution)/shard_map/all_gather | solution.py:78
  213.5 2.5 broadcast_select_fusion.1
  215.9 0.7 fusion.12
  216.6 1.1 multiply_reduce_fusion
  217.7 0.7 sqrt_select_fusion
  218.9 0.8 convolution_convert_fusion
  219.7 8.0 %reshape.102 = bf16[128,2,128,32]{3,2,1,0:T(8,128)(2,1)} reshape(bf16[256,4096]{1,0:T(8,128)(2,1)S(1)} %convolution_convert_fusion) | data formatting | bytes 4194304 | tf_op jit(solution)/shard_map/reshape | solution.py:89
  227.7 7.9 %copy.40 = bf16[128,2,128,32]{2,3,1,0:T(8,128)(2,1)} copy(bf16[128,2,128,32]{3,2,1,0:T(8,128)(2,1)} %reshape.102) | data formatting | bytes 4194304 | tf_op jit(solution)/shard_map/reshape | solution.py:89
  235.6 18.8 %all-to-all-start.1 = ((bf16[128,2,128,32]{2,3,1,0:T(8,128)(2,1)}), bf16[128,2,128,32]{2,3,1,0:T(8,128)(2,1)S(1)}, u32[]{:S(2)}, u32[]{:S(2)}) async-start(bf16[128,2,128,32]{2,3,1,0:T(8,128)(2,1)} %copy.40), calls=%async_computation.1 | async-start | bytes 4194304 | tf_op jit(solution)/shard_map/all_to_all | solution.py:90
  254.4 1.0 copy.42
  255.4 0.6 copy-done
  256.0 1.1 copy.43
  257.1 96.8 %all-to-all-done.1 = bf16[128,2,128,32]{2,3,1,0:T(8,128)(2,1)S(1)} async-done(((bf16[128,2,128,32]{2,3,1,0:T(8,128)(2,1)}), bf16[128,2,128,32]{2,3,1,0:T(8,128)(2,1)S(1)}, u32[]{:S(2)}, u32[]{:S(2)}) %all-to-all-start.1) | async-done | bytes 2097184 | tf_op jit(solution)/shard_map/all_to_all | solution.py:90
  353.8 1.2 gather_fusion
  (122 shorter events, 19.5 us)
Async XLA Ops:
  10.2 19.5 %copy-start.3 = (s32[256]{0:T(256)S(1)}, s32[256]{0:T(256)}, u32[]{:S(2)}) copy-start(s32[256]{0:T(256)} %param.6) | copy-start | bytes 3076
  10.2 118.8 %all-to-all-start = ((bf16[128,2,128,32]{2,3,1,0:T(8,128)(2,1)}), bf16[128,2,128,32]{2,3,1,0:T(8,128)(2,1)S(1)}, u32[]{:S(2)}, u32[]{:S(2)}) async-start(bf16[128,2,128,32]{2,3,1,0:T(8,128)(2,1)} %broadcast_select_fusion), calls=%async_computation | async-start | bytes 4194304 | tf_op jit(solution)/shard_map/all_to_all | solution.py:64
  29.7 183.8 %all-gather.2.cloned.1.call-start = ((), (), s32[]{:S(2)}) async-start(), calls=%async_computation.2 | async-start | bytes 1310720 | tf_op jit(solution)/shard_map/all_gather | solution.py:78
  146.2 12.0 %copy-start.2 = (f32[8,2,128,128]{3,2,1,0:T(8,128)S(1)}, f32[8,2,128,128]{3,2,1,0:T(8,128)}, u32[]{:S(2)}) copy-start(f32[8,2,128,128]{3,2,1,0:T(8,128)} %param.7) | copy-start | bytes 3145732
  213.5 3.1 copy-start.1
  235.6 118.2 %all-to-all-start.1 = ((bf16[128,2,128,32]{2,3,1,0:T(8,128)(2,1)}), bf16[128,2,128,32]{2,3,1,0:T(8,128)(2,1)S(1)}, u32[]{:S(2)}, u32[]{:S(2)}) async-start(bf16[128,2,128,32]{2,3,1,0:T(8,128)(2,1)} %copy.40), calls=%async_computation.1 | async-start | bytes 4194304 | tf_op jit(solution)/shard_map/all_to_all | solution.py:90
  254.4 1.6 copy-start
Sparse Core Ops, SparseCore 0:
  189.8 23.6 all-gather.1
where the time goes:
time: 363 us; the launch traced here: 362 us
  waiting for transfers between devices  218 us (60%)
  local copies, waits for them, and re-layouts  39.5 us (11%)
  starting transfers between devices  38.2 us (11%)
  matrix products  31.2 us (9%)
  between operations  14.2 us (4%)
  blocking collectives  10.7 us (3%)
  other arithmetic  8.89 us (2%)
    all_to_all x1, waiting for transfers between devices, per_device(): lax.all_to_all(route(grad_blocks), 'dp', split_axis=0, concat_axis=0, til...  97.5 us
    all_to_all x1, waiting for transfers between devices, per_device(): lax.all_to_all(outgoing, 'dp', split_axis=0, concat_axis=0, tiled=True)  96.8 us
    dot_general x64, matrix products, batch_product(): jnp.einsum('pij,pjk->pik', first, second, precision=lax.Precision.HIGHEST)  27.7 us
    all_gather x1, waiting for transfers between devices, per_device(): lax.all_gather(newton_roots(my_problems), 'mp', axis=0, tiled=True)  23.8 us
    all_to_all x1, starting transfers between devices, per_device(): lax.all_to_all(route(grad_blocks), 'dp', split_axis=0, concat_axis=0, til...  19.4 us
    all_to_all x1, starting transfers between devices, per_device(): lax.all_to_all(outgoing, 'dp', split_axis=0, concat_axis=0, tiled=True)  18.8 us
    reshape x2, local copies, waits for them, and re-layouts, per_device(): outgoing.astype(jnp.bfloat16)  15.9 us
    all_gather x1, blocking collectives, per_device(): whole = lax.all_gather(pick(arrived), 'mp', axis=2, tiled=True)  10.7 us
  transfers between devices with their start and end apart: 3, of which 3 were waited for; matrix products, arithmetic and copies ran while one was open for 1% of the time, Pallas kernels for 0%

commit v1 on v0

--- a/solution.py
+++ b/solution.py
@@ -75,7 +75,10 @@
     )
     share = 2 * capacity // part_count
     my_problems = lax.dynamic_slice_in_dim(problems, part_index * share, share, 0)
-    roots_flat = lax.all_gather(newton_roots(my_problems), "mp", axis=0, tiled=True)
+    roots_flat = jnp.concatenate(
+        lax.all_to_all(jnp.stack([newton_roots(my_problems)] * lax.axis_size("mp")), "mp", 0, 0),
+        axis=0,
+    )
     roots = roots_flat.reshape(capacity, 2, width, width)
     inv_roots = jnp.where(filled[:, None, None, None], roots, 0.0)
     whole_wide = whole.astype(jnp.float32)

time: 363 us -> 332 us (0.915)
  between operations: 14.2 us -> 0.84 us
  waiting for transfers between devices: 218 us -> 208 us
  starting transfers between devices: 38.2 us -> 32.2 us
    all_gather x1 -> x0, waiting for transfers between devices: 23.8 us -> none  [per_device(): lax.all_gather(newton_roots(my_problems), 'mp', axis=0, tiled=True)]
    all_to_all x0 -> x1, waiting for transfers between devices: none -> 13.4 us  [per_device(): lax.all_to_all(jnp.stack([newton_roots(my_problems)] * lax.axis_size('mp'...]
    all_to_all x1, starting transfers between devices: 18.8 us -> 9.29 us  [per_device(): lax.all_to_all(outgoing, 'dp', split_axis=0, concat_axis=0, tiled=True)]
where the time goes in v1:
time: 332 us; the launch traced here: 331 us
  waiting for transfers between devices  208 us (63%)
  local copies, waits for them, and re-layouts  39.9 us (12%)
  starting transfers between devices  32.2 us (10%)
  matrix products  31.2 us (9%)
  blocking collectives  10.7 us (3%)
  other arithmetic  7.59 us (2%)
    all_to_all x1, waiting for transfers between devices, per_device(): lax.all_to_all(route(grad_blocks), 'dp', split_axis=0, concat_axis=0, til...  97.5 us
    all_to_all x1, waiting for transfers between devices, per_device(): lax.all_to_all(outgoing, 'dp', split_axis=0, concat_axis=0, tiled=True)  96.8 us
    dot_general x64, matrix products, batch_product(): jnp.einsum('pij,pjk->pik', first, second, precision=lax.Precision.HIGHEST)  27.7 us
    all_to_all x1, starting transfers between devices, per_device(): lax.all_to_all(route(grad_blocks), 'dp', split_axis=0, concat_axis=0, til...  19.4 us
    reshape x2, local copies, waits for them, and re-layouts, per_device(): outgoing.astype(jnp.bfloat16)  15.9 us
    all_to_all x1, waiting for transfers between devices, per_device(): lax.all_to_all(jnp.stack([newton_roots(my_problems)] * lax.axis_size('mp'...  13.4 us
    all_gather x1, blocking collectives, per_device(): whole = lax.all_gather(pick(arrived), 'mp', axis=2, tiled=True)  10.7 us
    reshape x1, local copies, waits for them, and re-layouts, pick(): flat = arrived.reshape(block_total, -1)  10.7 us
  transfers between devices with their start and end apart: 3, of which 3 were waited for; matrix products, arithmetic and copies ran while one was open for 1% of the time, Pallas kernels for 0%

profile of v1, /device:TPU:33, one launch (start us, length us, event | category | flops | bytes accessed | tf_op | source)
XLA Modules:
  0.0 331.1 jit_solution(344616469350821097)
XLA Ops:
  0.6 0.8 fusion.27
  1.4 2.3 broadcast_select_fusion
  3.7 19.4 %all-to-all-start = ((bf16[128,2,128,32]{2,3,1,0:T(8,128)(2,1)}), bf16[128,2,128,32]{2,3,1,0:T(8,128)(2,1)S(1)}, u32[]{:S(2)}, u32[]{:S(2)}) async-start(bf16[128,2,128,32]{2,3,1,0:T(8,128)(2,1)} %broadcast_select_fusion), calls=%async_computation | async-start | bytes 4194304 | tf_op jit(solution)/shard_map/all_to_all | solution.py:64
  23.7 0.6 fusion.28
  24.3 0.6 iota_compare_fusion.4
  25.0 97.5 %all-to-all-done = bf16[128,2,128,32]{2,3,1,0:T(8,128)(2,1)S(1)} async-done(((bf16[128,2,128,32]{2,3,1,0:T(8,128)(2,1)}), bf16[128,2,128,32]{2,3,1,0:T(8,128)(2,1)S(1)}, u32[]{:S(2)}, u32[]{:S(2)}) %all-to-all-start) | async-done | bytes 2097184 | tf_op jit(solution)/shard_map/all_to_all | solution.py:64
  122.6 6.5 %copy.33 = bf16[128,2,128,32]{3,2,1,0:T(8,128)(2,1)} copy(bf16[128,2,128,32]{2,3,1,0:T(8,128)(2,1)S(1)} %all-to-all-done) | data formatting | bytes 4194304 | tf_op jit(solution)/shard_map/all_to_all | solution.py:64
  129.0 10.7 %reshape.96 = bf16[256,4096]{1,0:T(8,128)(2,1)S(1)} reshape(bf16[128,2,128,32]{3,2,1,0:T(8,128)(2,1)} %copy.33) | data formatting | bytes 4194304 | tf_op jit(solution)/shard_map/reshape | solution.py:60
  140.4 10.7 %all_gather.3 = bf16[8,128,128]{1,2,0:T(8,128)(2,1)S(1)} all-gather(bf16[8,128,32]{1,2,0:T(8,128)(2,1)S(1)} %copy.34), channel_id=1, replica_groups=mesh['dp'=128,'mp'=4] {'mp'}, dimensions={2}, use_global_device_ids=true | all-gather | bytes 327680 | tf_op jit(solution)/shard_map/all_gather | solution.py:65
  152.7 29.6 %while.13 = (s32[]{:T(128)}, f32[4,128,128]{1,2,0:T(8,128)S(1)}, f32[4,128,128]{2,1,0:T(8,128)S(1)}, s32[]{:T(128)}) while((s32[]{:T(128)}, f32[4,128,128]{1,2,0:T(8,128)S(1)}, f32[4,128,128]{2,1,0:T(8,128)S(1)}, s32[]{:T(128)}) %tuple.39), condition=%wide.region_6.7_spmd.clone, body=%wide.region_5.6_spmd.clone.sunk | while | flops 402948096 | bytes 3866677 | solution.py:32
  153.5 0.6 convolution_bitcast_fusion.4
  154.1 0.4 fusion.63
  155.4 0.6 convolution_bitcast_fusion.4
  156.0 0.4 fusion.63
  157.2 0.6 convolution_bitcast_fusion.4
  159.1 0.6 convolution_bitcast_fusion.4
  160.9 0.6 convolution_bitcast_fusion.4
  161.5 0.4 fusion.63
  162.8 0.6 convolution_bitcast_fusion.4
  164.6 0.6 convolution_bitcast_fusion.4
  166.4 0.6 convolution_bitcast_fusion.4
  167.1 0.4 fusion.63
  168.3 0.6 convolution_bitcast_fusion.4
  170.1 0.6 convolution_bitcast_fusion.4
  170.8 0.4 fusion.63
  172.0 0.6 convolution_bitcast_fusion.4
  173.8 0.6 convolution_bitcast_fusion.4
  175.7 0.6 convolution_bitcast_fusion.4
  177.5 0.6 convolution_bitcast_fusion.4
  178.1 0.4 fusion.63
  179.4 0.6 convolution_bitcast_fusion.4
  181.2 0.6 convolution_bitcast_fusion.4
  182.4 1.1 stack.19
  183.5 3.5 %all-to-all-start.1 = ((f32[4,4,128,128]{3,2,1,0:T(8,128)}), f32[4,4,128,128]{3,2,1,0:T(8,128)S(1)}, u32[]{:S(2)}, u32[]{:S(2)}) async-start(f32[4,4,128,128]{3,2,1,0:T(8,128)} %stack.19), calls=%async_computation.1 | async-start | bytes 2097152 | tf_op jit(solution)/shard_map/all_to_all | solution.py:79
  187.0 13.4 %all-to-all-done.1 = f32[4,4,128,128]{3,2,1,0:T(8,128)S(1)} async-done(((f32[4,4,128,128]{3,2,1,0:T(8,128)}), f32[4,4,128,128]{3,2,1,0:T(8,128)S(1)}, u32[]{:S(2)}, u32[]{:S(2)}) %all-to-all-start.1) | async-done | bytes 1048608 | tf_op jit(solution)/shard_map/all_to_all | solution.py:79
  200.4 1.2 broadcast_select_fusion.1
  201.5 0.7 fusion.12
  202.2 1.1 multiply_reduce_fusion
  203.3 0.7 sqrt_select_fusion
  204.5 0.8 convolution_convert_fusion
  205.3 8.0 %reshape.100 = bf16[128,2,128,32]{3,2,1,0:T(8,128)(2,1)} reshape(bf16[256,4096]{1,0:T(8,128)(2,1)S(1)} %convolution_convert_fusion) | data formatting | bytes 4194304 | tf_op jit(solution)/shard_map/reshape | solution.py:92
  213.3 7.9 %copy.41 = bf16[128,2,128,32]{2,3,1,0:T(8,128)(2,1)} copy(bf16[128,2,128,32]{3,2,1,0:T(8,128)(2,1)} %reshape.100) | data formatting | bytes 4194304 | tf_op jit(solution)/shard_map/reshape | solution.py:92
  221.2 9.3 %all-to-all-start.2 = ((bf16[128,2,128,32]{2,3,1,0:T(8,128)(2,1)}), bf16[128,2,128,32]{2,3,1,0:T(8,128)(2,1)S(1)}, u32[]{:S(2)}, u32[]{:S(2)}) async-start(bf16[128,2,128,32]{2,3,1,0:T(8,128)(2,1)} %copy.41), calls=%async_computation.2 | async-start | bytes 4194304 | tf_op jit(solution)/shard_map/all_to_all | solution.py:93
  230.5 1.1 copy.43
  231.6 0.5 copy-done
  232.1 1.1 copy.44
  233.2 96.8 %all-to-all-done.2 = bf16[128,2,128,32]{2,3,1,0:T(8,128)(2,1)S(1)} async-done(((bf16[128,2,128,32]{2,3,1,0:T(8,128)(2,1)}), bf16[128,2,128,32]{2,3,1,0:T(8,128)(2,1)S(1)}, u32[]{:S(2)}, u32[]{:S(2)}) %all-to-all-start.2) | async-done | bytes 2097184 | tf_op jit(solution)/shard_map/all_to_all | solution.py:93
  329.9 1.2 gather_fusion
  (120 shorter events, 20.0 us)
Async XLA Ops:
  3.7 19.4 %copy-start.2 = (s32[256]{0:T(256)S(1)}, s32[256]{0:T(256)}, u32[]{:S(2)}) copy-start(s32[256]{0:T(256)} %param.6) | copy-start | bytes 3076
  3.7 118.8 %all-to-all-start = ((bf16[128,2,128,32]{2,3,1,0:T(8,128)(2,1)}), bf16[128,2,128,32]{2,3,1,0:T(8,128)(2,1)S(1)}, u32[]{:S(2)}, u32[]{:S(2)}) async-start(bf16[128,2,128,32]{2,3,1,0:T(8,128)(2,1)} %broadcast_select_fusion), calls=%async_computation | async-start | bytes 4194304 | tf_op jit(solution)/shard_map/all_to_all | solution.py:64
  140.1 11.6 %copy-start.1 = (f32[8,2,128,128]{3,2,1,0:T(8,128)S(1)}, f32[8,2,128,128]{3,2,1,0:T(8,128)}, u32[]{:S(2)}) copy-start(f32[8,2,128,128]{3,2,1,0:T(8,128)} %param.7) | copy-start | bytes 3145732
  183.5 16.9 %all-to-all-start.1 = ((f32[4,4,128,128]{3,2,1,0:T(8,128)}), f32[4,4,128,128]{3,2,1,0:T(8,128)S(1)}, u32[]{:S(2)}, u32[]{:S(2)}) async-start(f32[4,4,128,128]{3,2,1,0:T(8,128)} %stack.19), calls=%async_computation.1 | async-start | bytes 2097152 | tf_op jit(solution)/shard_map/all_to_all | solution.py:79
  221.2 108.7 %all-to-all-start.2 = ((bf16[128,2,128,32]{2,3,1,0:T(8,128)(2,1)}), bf16[128,2,128,32]{2,3,1,0:T(8,128)(2,1)S(1)}, u32[]{:S(2)}, u32[]{:S(2)}) async-start(bf16[128,2,128,32]{2,3,1,0:T(8,128)(2,1)} %copy.41), calls=%async_computation.2 | async-start | bytes 4194304 | tf_op jit(solution)/shard_map/all_to_all | solution.py:93
  230.5 1.6 copy-start
